TPU v7x, 32 devices: a whole 2x2x4 slice. The times are simulated.
32 devices in a mesh: groups: 2 (over x), seq: 8 (over z, y), mp: 2 (over core).
Axes of the slice: x: 2, y: 2, z: 4, core: 2. Of those that a mesh axis runs over, the one named last changes fastest.
Arguments:
- latent_cache: bfloat16 [2048, 64, 512], P(('groups', 'seq')), parts along dimension 0, may hold values from -6 to 6
- rope_cache: bfloat16 [2048, 4096], P(('groups', 'seq')), parts along dimension 0, may hold values from -6 to 6
- q_nope: bfloat16 [16, 128, 128], P('groups', 'mp'), parts along dimension 0, may hold values from -12 to 12
- q_rope: bfloat16 [16, 128, 64], P('groups', 'mp'), parts along dimension 0, may hold values from -2000 to 2000
- w_uk: bfloat16 [128, 128, 512], P('mp', None, 'seq'), may hold values from -0.5 to 0.5
- value_up_weight: bfloat16 [128, 512, 128], P('mp', 'seq'), may hold values from -0.25 to 0.25
- w_out: bfloat16 [16384, 7168], P('mp', 'seq'), may hold values from -0.046875 to 0.046875
- page_table: int32 [16, 256], P('groups'), parts along dimension 0, may hold values from 0 to 1023, as said below
- lengths: int32 [16], P('groups'), parts along dimension 0, may hold values from 2048 to 16384, as said below
Outputs:
- output: bfloat16 [16, 7168], P('groups', ('seq', 'mp')), parts along dimension 0
There are 2 independent parts, one for each index of `groups`. A program takes and returns all parts, laid end to end along the dimension named above; an argument that names none is the same for every part. Nothing has to cross between parts.
Inputs may be any that keep to these rules, and one draw needn't show every extreme that they name: `lengths`: every sequence has one eighth of 16384 tokens or more; the longest has exactly 16384. page_table[b,p] for p < ceil(lengths[b] / 64) is the global slot (shard index times 128 plus local slot) holding that page; these live entries are all distinct; the other entries are 0 and unused.
All inputs are finite; a program needn't handle non-finite values.
Results may differ from a plain program's by a relative error of at most 0.012.
Values may be sent and summed in bfloat16 or wider, within the bound.
A program may use at most 128 MiB of HBM per device.

v0:
```python
import functools

import jax
import jax.numpy as jnp
from jax import lax
from jax.experimental import pallas as pl
from jax.experimental.pallas import tpu as pltpu
from jax.sharding import PartitionSpec as P

NEG = -1e30
MESH = pl.DeviceIdType.MESH
GROUP = 8
F32 = jnp.float32
BF16 = jnp.bfloat16


def greet(n, me, partner=None):
    barrier = pltpu.get_barrier_semaphore()
    for k in range(1, n):
        peer = lax.rem(me + k, n)
        pl.semaphore_signal(barrier, inc=1, device_id={"seq": peer}, device_id_type=MESH)
    if partner is not None:
        pl.semaphore_signal(barrier, inc=1, device_id={"mp": partner}, device_id_type=MESH)
    pl.semaphore_wait(barrier, n - 1 + (partner is not None))


def push(n, me, src_of, dst, send, recv):
    copies = []
    for k in range(1, n):
        peer = lax.rem(me + k, n)
        copy = pltpu.make_async_remote_copy(
            src_ref=src_of(peer), dst_ref=dst.at[me], send_sem=send.at[k], recv_sem=recv.at[k],
            device_id={"seq": peer}, device_id_type=MESH,
        )
        copy.start()
        copies.append(copy)
    return copies


def make_plan(first_slot, page, most, lengths_ref, table_ref, plan_ref):
    seqs, pages = table_ref.shape
    slots_dev, wide = most
    table = table_ref[...].astype(F32).T
    logical = lax.broadcasted_iota(jnp.int32, (pages, 1), 0)
    slot = lax.broadcasted_iota(jnp.int32, (pages, slots_dev), 1) + first_slot
    slot = slot.astype(F32)
    fill = []
    for b in range(seqs):
        inside = jnp.clip(lengths_ref[b] - page * logical, 0, page)
        hit = table[:, b:b + 1] == slot
        fill.append(jnp.sum(jnp.where(hit, inside, 0), axis=0, keepdims=True))
    eye = (lax.broadcasted_iota(jnp.int32, (slots_dev, slots_dev), 0)
           == lax.broadcasted_iota(jnp.int32, (slots_dev, slots_dev), 1))
    earlier = (lax.broadcasted_iota(jnp.int32, (slots_dev, slots_dev), 1)
               < lax.broadcasted_iota(jnp.int32, (slots_dev, slots_dev), 0))
    at = lax.broadcasted_iota(jnp.int32, (1, wide), 1)
    start = jnp.zeros((1, 1), jnp.int32)
    owner = jnp.zeros((1, wide), jnp.int32)
    target = jnp.full((slots_dev, 1), -1, jnp.int32)
    column = jnp.zeros((slots_dev, 1), jnp.int32)
    for b in range(seqs):
        owned = fill[b] > 0
        count = jnp.sum(owned.astype(jnp.int32), axis=1, keepdims=True)
        place = jnp.sum(jnp.where(earlier & owned, 1, 0), axis=1, keepdims=True)
        mine = jnp.sum(jnp.where(eye, fill[b], 0), axis=1, keepdims=True)
        target = jnp.where(mine > 0, start * GROUP + place, target)
        column = column + mine
        start = start + (count + GROUP - 1) // GROUP
        owner = owner + (at >= start).astype(jnp.int32)
    match = target == lax.broadcasted_iota(jnp.int32, (slots_dev, wide), 1)
    ids = lax.broadcasted_iota(jnp.int32, (slots_dev, wide), 0)
    plan_ref[0:1, :] = jnp.sum(jnp.where(match, ids, 0), axis=0, keepdims=True)
    plan_ref[1:2, :] = jnp.sum(jnp.where(match, column, 0), axis=0, keepdims=True)
    plan_ref[2:3, :] = jnp.minimum(owner, seqs - 1)
    plan_ref[3:4, :] = jnp.broadcast_to(start, (1, wide))
    plan_ref[4:8, :] = jnp.zeros((4, wide), jnp.int32)


def query_kernel(n, pack, page, lengths_ref, table_ref, rope_ref, q_ref, w_ref, out_ref, plan_ref, spread_ref,
                 raw, flat, gath, wide_rope, send, recv, send2, recv2):
    me = lax.axis_index("seq")
    seqs, heads, _ = q_ref.shape
    cols = w_ref.shape[1]
    partner = me + 1 - 2 * lax.rem(me, 2)
    barrier = pltpu.get_barrier_semaphore()
    for peer in [lax.rem(me + 2 * k, n) for k in range(1, n // 2)] + [partner]:
        pl.semaphore_signal(barrier, inc=1, device_id={"seq": peer}, device_id_type=MESH)
    for b in range(seqs):
        flat[b * heads:(b + 1) * heads, :] = q_ref[b].astype(F32)
    for h in range(heads):
        q = flat[pl.ds(h, seqs, stride=heads), :].astype(BF16)
        raw[h * seqs:(h + 1) * seqs, :] = lax.dot_general(
            q, w_ref[h], (((1,), (1,)), ((), ())), preferred_element_type=F32)
    for b in range(0, seqs, pack):
        parts = [raw[pl.ds(b + j, heads, stride=seqs), :] for j in range(pack)]
        row = parts[0] if pack == 1 else jnp.concatenate(parts, axis=1)
        gath[me, b // pack * heads:(b // pack + 1) * heads, :] = row.astype(BF16)
    pl.semaphore_wait(barrier, n // 2)

    def send_to(block, peer, s, r):
        copy = pltpu.make_async_remote_copy(
            src_ref=gath.at[block], dst_ref=gath.at[block], send_sem=s, recv_sem=r,
            device_id={"seq": peer}, device_id_type=MESH)
        copy.start()
        return copy

    across = [send_to(me, partner, send2.at[0], recv2.at[0])]
    line = [send_to(me, lax.rem(me + 2 * k, n), send.at[k], recv.at[k]) for k in range(1, n // 2)]

    slots_dev = rope_ref.shape[0]
    make_plan(me * slots_dev, page, (slots_dev, plan_ref.shape[1]), lengths_ref, table_ref, plan_ref)
    per = page * 128 // rope_ref.shape[1]
    lane = lax.broadcasted_iota(jnp.int32, (slots_dev, 128), 1) // (128 // per)
    for i in range(rope_ref.shape[1] // 128):
        x = rope_ref[:, i * 128:(i + 1) * 128].astype(F32)
        for j in range(per):
            wide_rope[pl.ds(i * per + j, slots_dev, stride=page), :] = jnp.where(lane == j, x, 0.0)

    def narrow(i, _):
        spread_ref[i] = wide_rope[pl.ds(pl.multiple_of(i * page, page), page), :].astype(BF16)
        return 0

    lax.fori_loop(0, slots_dev, narrow, 0, unroll=4)

    for k in range(1, n // 2):
        line[k - 1].wait_recv()
        across.append(send_to(lax.rem(me - 2 * k + n, n), partner, send2.at[k], recv2.at[k]))
    for copy in line:
        copy.wait_send()
    for copy in across:
        copy.wait()
    for s in range(n):
        for b in range(seqs):
            at = b % pack * cols
            out_ref[b, :, s * cols:(s + 1) * cols] = gath[
                s, b // pack * heads:(b // pack + 1) * heads, at:at + cols]


def attend_kernel(scale, pack, plan_ref, q_ref, qr_ref, rope_ref, latent_ref,
                  out_ref, kbuf, acc, top, total, turn, ready, sems):
    seqs, heads, width = q_ref.shape
    page = latent_ref.shape[1]
    tokens = GROUP * page
    n = out_ref.shape[0]
    cols = width // n
    count = plan_ref[3, 0]
    acc[...] = jnp.zeros_like(acc)
    top[...] = jnp.full(top.shape, NEG, F32)
    total[...] = jnp.zeros_like(total)

    def fetch(c, buf):
        return [pltpu.make_async_copy(
            latent_ref.at[plan_ref[0, c * GROUP + g]], kbuf.at[buf, pl.ds(g * page, page)], sems.at[buf, g])
            for g in range(GROUP)]

    for ahead in range(3):
        @pl.when(count > ahead)
        def _():
            for copy in fetch(ahead, ahead):
                copy.start()

    lane = lax.broadcasted_iota(jnp.int32, (1, tokens), 1)

    for b in range(seqs):
        turn[b] = jnp.concatenate([qr_ref[b]] * (128 // qr_ref.shape[2]), axis=1)

    def score_of(c):
        b = plan_ref[2, c]
        rope = jnp.concatenate([rope_ref[plan_ref[0, c * GROUP + g]] for g in range(GROUP)], axis=0)
        limit = jnp.zeros((1, tokens), jnp.int32)
        for g in range(GROUP):
            limit = jnp.where(lane // page == g, plan_ref[1, c * GROUP + g] + g * page, limit)
        nt = (((1,), (1,)), ((), ()))
        score = lax.dot_general(turn[b], rope, nt, preferred_element_type=F32)
        keys = kbuf[lax.rem(c, 4)]
        score = (score + lax.dot_general(q_ref[b], keys, nt, preferred_element_type=F32)) * scale
        return jnp.where(lane < limit, score, NEG)

    @pl.when(count > 0)
    def _():
        for copy in fetch(0, 0):
            copy.wait()
        ready[...] = score_of(0)

    def step(c, _):
        @pl.when(c + 3 < count)
        def _():
            for copy in fetch(c + 3, lax.rem(c + 3, 4)):
                copy.start()

        @pl.when(c + 1 < count)
        def _():
            for copy in fetch(c + 1, lax.rem(c + 1, 4)):
                copy.wait()

        score = ready[...]
        upcoming = score_of(c + 1)
        b = plan_ref[2, c]
        keys = kbuf[lax.rem(c, 4)]
        old = top[b][:, :1]
        new = jnp.maximum(old, jnp.max(score, axis=1, keepdims=True))
        weight = jnp.exp(score - new)
        carry = jnp.exp(old - new)
        product = jnp.dot(weight.astype(BF16), keys, preferred_element_type=F32)
        total[b] = total[b] * carry + jnp.sum(weight, axis=1, keepdims=True)
        top[b] = jnp.broadcast_to(new, top.shape[1:])
        acc[b] = acc[b] * carry + product
        ready[...] = upcoming
        return 0

    lax.fori_loop(0, count, step, 0)

    ids = lax.broadcasted_iota(jnp.int32, (heads, 128), 1)
    extra = jnp.zeros((heads, 128), F32)
    for b in range(seqs):
        inv = 1.0 / jnp.maximum(total[b][:, :1], 1e-30)
        whole = acc[b] * inv
        for s in range(n):
            at = b % pack * cols
            out_ref[s, b // pack * heads:(b // pack + 1) * heads, at:at + cols] = whole[
                :, s * cols:(s + 1) * cols].astype(BF16)
        for k, value in enumerate((top[b], total[b])):
            for j in range(3):
                term = value.astype(BF16).astype(F32)
                extra = jnp.where(ids == (k * 3 + j) * seqs + b, term, extra)
                value = value - term
    base = seqs // pack * heads
    lanes = out_ref.shape[2]
    for s in range(n):
        out_ref[s, base:base + heads, :] = extra[:, :lanes].astype(BF16)


def finish_kernel(n, pack, o_ref, v_ref, w_hbm, out_ref, gath, port, pv, part, vals, lhs, w_buf, res,
                  tx, rx, send1, recv1, send2, recv2, send3, recv3, send4, recv4, wsem):
    me = lax.axis_index("seq")
    half = lax.axis_index("mp")
    heads, cols, vdim = v_ref.shape
    seqs = lhs.shape[0]
    hs = heads // n
    load = pltpu.make_async_copy(w_hbm, w_buf, wsem)
    load.start()
    greet(n, me, 1 - half)
    copies = push(n, me, lambda peer: o_ref.at[peer], gath, send1, recv1)
    gath[me] = o_ref[me]
    for copy in copies:
        copy.wait()

    base = seqs // pack * heads
    tops, sums = [], []
    for s in range(n):
        e = gath[s, base:base + heads, :].astype(F32)
        terms = [e[:, k * seqs:(k + 1) * seqs] for k in range(6)]
        tops.append(terms[0] + terms[1] + terms[2])
        sums.append(terms[3] + terms[4] + terms[5])
    best = functools.reduce(jnp.maximum, tops)
    shares = [x * jnp.exp(t - best) for t, x in zip(tops, sums)]
    inv = 1.0 / functools.reduce(jnp.add, shares)
    shares = [x * inv for x in shares]
    lane = lax.broadcasted_iota(jnp.int32, (heads, pack * cols), 1) // cols
    for p in range(seqs // pack):
        total = jnp.zeros((heads, pack * cols), F32)
        for s in range(n):
            share = jnp.broadcast_to(shares[s][:, p * pack:p * pack + 1], total.shape)
            for j in range(1, pack):
                share = jnp.where(lane == j, shares[s][:, p * pack + j:p * pack + j + 1], share)
            total = total + gath[s, p * heads:(p + 1) * heads, :].astype(F32) * share
        for j in range(pack):
            b = p * pack + j
            port[b * heads:(b + 1) * heads, :] = total[:, j * cols:(j + 1) * cols]
    for h in range(heads):
        x = port[pl.ds(h, seqs, stride=heads), :].astype(BF16)
        pv[h // hs, h % hs * seqs:(h % hs + 1) * seqs, :] = jnp.dot(
            x, v_ref[h], preferred_element_type=F32).astype(BF16)
    copies = push(n, me, lambda peer: pv.at[peer], part, send2, recv2)
    part[me] = pv[me]
    for copy in copies:
        copy.wait()
    total = part[0].astype(F32)
    for s in range(1, n):
        total = total + part[s].astype(F32)
    vals[me] = total.astype(BF16)
    copies = push(n, me, lambda peer: vals.at[me], vals, send3, recv3)
    load.wait()
    rows = hs * vdim
    for k in range(n):
        src = lax.rem(me - k + n, n)
        if k:
            copies[k - 1].wait_recv()
        for h in range(hs):
            lhs[:, h * vdim:(h + 1) * vdim] = vals[src, h * seqs:(h + 1) * seqs, :]
        at = pl.ds(pl.multiple_of(src * rows, rows), rows)
        product = jnp.dot(lhs[...], w_buf[at, :], preferred_element_type=F32)
        if k:
            res[...] += product
        else:
            res[...] = product
    for copy in copies:
        copy.wait_send()
    wide = res.shape[1] // 2
    low, high = res[:, :wide], res[:, wide:]
    first = half == 0
    tx[...] = jnp.where(first, high, low)
    copy = pltpu.make_async_remote_copy(
        src_ref=tx, dst_ref=rx, send_sem=send4, recv_sem=recv4,
        device_id={"mp": 1 - half}, device_id_type=MESH)
    copy.start()
    copy.wait()
    out_ref[...] = (jnp.where(first, low, high) + rx[...]).astype(BF16)


def local(n, latent_cache, rope_cache, q_nope, q_rope, w_uk, value_up_weight, w_out, page_table, lengths):
    slots_dev, page, width = latent_cache.shape
    seqs, heads, nope = q_nope.shape
    rope_w = q_rope.shape[2]
    cols = w_uk.shape[2]
    vdim = value_up_weight.shape[2]
    scale = (nope + rope_w) ** (-0.5)
    pack = max(1, min(seqs, 128 // cols))
    lanes = pack * cols
    vm = pl.BlockSpec(memory_space=pltpu.VMEM)
    sm = pl.BlockSpec(memory_space=pltpu.SMEM)
    hbm = pl.BlockSpec(memory_space=pl.ANY)
    dma = pltpu.SemaphoreType.DMA
    params = functools.partial(pltpu.CompilerParams, has_side_effects=True)

    most = (slots_dev + seqs * (GROUP - 1)) // GROUP * GROUP
    q_latent, steps, rope = pl.pallas_call(
        functools.partial(query_kernel, n, pack, page),
        out_shape=(
            jax.ShapeDtypeStruct((seqs, heads, width), BF16),
            jax.ShapeDtypeStruct((8, (most + GROUP + 127) // 128 * 128), jnp.int32),
            jax.ShapeDtypeStruct((slots_dev, page, 128), BF16),
        ),
        in_specs=[sm, vm, vm, vm, vm], out_specs=(vm, vm, vm),
        scratch_shapes=[
            pltpu.VMEM((heads * seqs, cols), F32),
            pltpu.VMEM((heads * seqs, nope), F32),
            pltpu.VMEM((n, seqs // pack * heads, lanes), BF16),
            pltpu.VMEM((slots_dev * page, 128), F32),
            dma((n // 2,)), dma((n // 2,)), dma((n // 2,)), dma((n // 2,)),
        ],
        compiler_params=params(collective_id=1, vmem_limit_bytes=58 * 1024 * 1024), name="queries",
    )(lengths, page_table, rope_cache, q_nope, w_uk.transpose(0, 2, 1))

    rows = seqs // pack * heads + heads
    mixed = pl.pallas_call(
        functools.partial(attend_kernel, scale, pack),
        out_shape=jax.ShapeDtypeStruct((n, rows, lanes), BF16),
        in_specs=[sm, vm, vm, vm, hbm], out_specs=vm,
        scratch_shapes=[
            pltpu.VMEM((4, GROUP * page, width), BF16),
            pltpu.VMEM((seqs, heads, width), F32),
            pltpu.VMEM((seqs, heads, 128), F32),
            pltpu.VMEM((seqs, heads, 128), F32),
            pltpu.VMEM((seqs, heads, 128), BF16),
            pltpu.VMEM((heads, GROUP * page), F32),
            dma((4, GROUP)),
        ],
        compiler_params=pltpu.CompilerParams(vmem_limit_bytes=58 * 1024 * 1024),
        name="attend",
    )(steps, q_latent, q_rope, rope, latent_cache)

    wide = w_out.shape[1]
    hs = heads // n
    return pl.pallas_call(
        functools.partial(finish_kernel, n, pack),
        out_shape=jax.ShapeDtypeStruct((seqs, wide // 2), BF16),
        in_specs=[vm, vm, hbm], out_specs=vm,
        scratch_shapes=[
            pltpu.VMEM((n, rows, lanes), BF16),
            pltpu.VMEM((seqs * heads, cols), F32),
            pltpu.VMEM((n, hs * seqs, vdim), BF16),
            pltpu.VMEM((n, hs * seqs, vdim), BF16),
            pltpu.VMEM((n, hs * seqs, vdim), BF16),
            pltpu.VMEM((seqs, hs * vdim), BF16),
            pltpu.VMEM(w_out.shape, BF16),
            pltpu.VMEM((seqs, wide), F32),
            pltpu.VMEM((seqs, wide // 2), F32),
            pltpu.VMEM((seqs, wide // 2), F32),
            dma((n,)), dma((n,)), dma((n,)), dma((n,)), dma((n,)), dma((n,)), dma, dma, dma,
        ],
        compiler_params=params(collective_id=2, vmem_limit_bytes=58 * 1024 * 1024), name="finish",
    )(mixed, value_up_weight, w_out)


def solution(mesh):
    return jax.shard_map(
        functools.partial(local, mesh.shape["seq"]),
        mesh=mesh,
        in_specs=(
            P(("groups", "seq"), None, None),
            P(("groups", "seq"), None),
            P("groups", "mp", None),
            P("groups", "mp", None),
            P("mp", None, "seq"),
            P("mp", "seq", None),
            P("mp", "seq"),
            P("groups", None),
            P("groups"),
        ),
        out_specs=P("groups", ("seq", "mp")),
        check_vma=False,
    )
```

profile of v0, /device:TPU:0, one launch (start us, length us, event | category | flops | bytes accessed | tf_op | source)
XLA Modules:
  0.0 70.0 jit_solution(7909092339813670737)
XLA Ops:
  0.0 20.2 %queries.1 = (bf16[8,64,512]{2,1,0:T(8,128)(2,1)}, s32[8,256]{1,0:T(8,128)}, bf16[128,64,128]{2,1,0:T(8,128)(2,1)}) custom-call(s32[8]{0:T(128)} %lengths_ref.1, s32[8,256]{1,0:T(8,128)} %table_ref.1, bf16[128,4096]{1,0:T(8,128)(2,1)} %rope_ref.1, bf16[8,64,128]{2,1,0:T(8,128)(2,1)} %q_ref.1, bf16[64,64,128]{2,1,0:T(8,128)(2,1)} %bitcast.1), custom_call_target="tpu_custom_call" | custom-call | tf_op jit(solution)/shard_map/queries/pallas_call | solution.py:327
  20.2 14.6 %attend.1.o_ref = bf16[8,320,128]{2,1,0:T(8,128)(2,1)} custom-call(s32[8,256]{1,0:T(8,128)} %get-tuple-element.8.plan_ref, bf16[8,64,512]{2,1,0:T(8,128)(2,1)} %get-tuple-element.9.q_ref, bf16[8,64,64]{2,1,0:T(8,128)(2,1)} %qr_ref.1, bf16[128,64,128]{2,1,0:T(8,128)(2,1)} %get-tuple-element.10.rope_ref, bf16[128,64,512]{2,1,0:T(8,128)(2,1)} %latent_ref.1), custom_call_target="tpu_custom_call" | custom-call | tf_op jit(solution)/shard_map/attend/pallas_call | solution.py:346
  34.8 33.9 %finish.1 = bf16[8,448]{1,0:T(8,128)(2,1)} custom-call(bf16[8,320,128]{2,1,0:T(8,128)(2,1)} %attend.1.o_ref, bf16[64,64,128]{2,1,0:T(8,128)(2,1)} %v_ref.1, bf16[8192,896]{1,0:T(8,128)(2,1)} %w_hbm.1), custom_call_target="tpu_custom_call" | custom-call | tf_op jit(solution)/shard_map/finish/pallas_call | solution.py:365
  68.8 1.3 %copy.11 = bf16[8,448]{1,0:T(8,128)(2,1)} copy(bf16[8,448]{1,0:T(8,128)(2,1)} %finish.1) | data formatting | bytes 14336
where the time goes:
time: 69.9 us; the launch traced here: 70 us
  Pallas kernels  68.7 us (98%)
  local copies, waits for them, and re-layouts  1.3 us (2%)
    pallas_call x1, Pallas kernels, local(): pl.pallas_call(functools.partial(finish_kernel, n, pack), out_shape=jax.S...  33.9 us
    pallas_call x1, Pallas kernels, local(): pl.pallas_call(functools.partial(query_kernel, n, pack, page), out_shape=...  20.2 us
    pallas_call x1, Pallas kernels, local(): pl.pallas_call(functools.partial(attend_kernel, scale, pack), out_shape=j...  14.6 us

commit v1 on v0

v1 whole, which is shorter than its diff:
```python
import functools

import jax
import jax.numpy as jnp
from jax import lax
from jax.experimental import pallas as pl
from jax.experimental.pallas import tpu as pltpu
from jax.sharding import PartitionSpec as P

NEG = -1e30
MESH = pl.DeviceIdType.MESH
GROUP = 4
UNROLL = 2
QPARTS = 2
F32 = jnp.float32
BF16 = jnp.bfloat16


def make_plan(first_slot, page, lengths_ref, table_ref, plan_ref):
    seqs, pages = table_ref.shape
    slots_dev, wide = first_slot[1], plan_ref.shape[1]
    table = table_ref[...].astype(F32).T
    logical = lax.broadcasted_iota(jnp.int32, (pages, 1), 0)
    slot = lax.broadcasted_iota(jnp.int32, (pages, slots_dev), 1) + first_slot[0]
    slot = slot.astype(F32)
    fill = []
    for b in range(seqs):
        inside = jnp.clip(lengths_ref[b] - page * logical, 0, page)
        hit = table[:, b:b + 1] == slot
        fill.append(jnp.sum(jnp.where(hit, inside, 0), axis=0, keepdims=True))
    eye = (lax.broadcasted_iota(jnp.int32, (slots_dev, slots_dev), 0)
           == lax.broadcasted_iota(jnp.int32, (slots_dev, slots_dev), 1))
    earlier = (lax.broadcasted_iota(jnp.int32, (slots_dev, slots_dev), 1)
               < lax.broadcasted_iota(jnp.int32, (slots_dev, slots_dev), 0))
    at = lax.broadcasted_iota(jnp.int32, (1, wide), 1)
    start = jnp.zeros((1, 1), jnp.int32)
    owner = jnp.zeros((1, wide), jnp.int32)
    fresh = jnp.zeros((1, wide), jnp.int32)
    entry = jnp.zeros((1, wide), jnp.int32)
    target = jnp.full((slots_dev, 1), -1, jnp.int32)
    column = jnp.zeros((slots_dev, 1), jnp.int32)
    for b in range(seqs):
        owned = fill[b] > 0
        count = jnp.sum(owned.astype(jnp.int32), axis=1, keepdims=True)
        place = jnp.sum(jnp.where(earlier & owned, 1, 0), axis=1, keepdims=True)
        mine = jnp.sum(jnp.where(eye, fill[b], 0), axis=1, keepdims=True)
        target = jnp.where(mine > 0, start * GROUP + place, target)
        column = column + mine
        fresh = jnp.where(at == start, 1, fresh)
        start = start + (count + GROUP - 1) // GROUP
        owner = owner + (at >= start).astype(jnp.int32)
        entry = jnp.where((at == b) & (count > 0), start, entry)
    match = target == lax.broadcasted_iota(jnp.int32, (slots_dev, wide), 1)
    ids = lax.broadcasted_iota(jnp.int32, (slots_dev, wide), 0)
    plan_ref[0:1, :] = jnp.sum(jnp.where(match, ids, 0), axis=0, keepdims=True)
    plan_ref[1:2, :] = jnp.sum(jnp.where(match, column, 0), axis=0, keepdims=True)
    plan_ref[2:3, :] = jnp.minimum(owner, seqs - 1)
    plan_ref[3:4, :] = fresh
    plan_ref[4:5, :] = entry
    plan_ref[5:8, :] = jnp.zeros((3, wide), jnp.int32)


def merge(seqs, stats, parts):
    hs = stats[0].shape[0] // 2
    tops = [s[:hs] for s in stats]
    best = functools.reduce(jnp.maximum, tops)
    shares = [s[hs:] * jnp.exp(t - best) for s, t in zip(stats, tops)]
    total = functools.reduce(jnp.add, shares)
    inv = 1.0 / jnp.maximum(total, 1e-30)
    out = None
    for share, part in zip(shares, parts):
        share = share * inv
        column = jnp.concatenate([share[:, b:b + 1] for b in range(seqs)], axis=0)
        term = part * column
        out = term if out is None else out + term
    return out, best, total


def kernel(n, groups, pack, scale, nch,
           lengths_hbm, table_hbm, rope_hbm, qn_hbm, wuk_hbm, qr_hbm, lat_hbm, v_hbm, w_hbm, out_ref,
           lengths, table, rope, qn, wuk, qr, lat, w_buf, plan_v, plan, raw, flat, gath, q_all, turn,
           wide_rope, spread, run, tops, sums, ready, mix, st, ygot, yst, zout, zst, zgot, zgst, port,
           vbuf, vals, tx, rx,
           lsem, bulk, qs1, qr1, qs2, qr2, vs1, vr1, vs2, vr2, ys, yr, yss, ysr, zs, zr, zss, zsr, as_, ar, ms, mr):
    me = lax.axis_index("seq")
    half = lax.axis_index("mp")
    grp = lax.axis_index("groups")
    seqs, heads, _ = qn.shape
    cols = wuk.shape[1]
    slots, page, width = lat.shape
    hs = heads // n
    line = n // 2
    par = lax.rem(me, 2)
    row = me // 2
    partner = me + 1 - 2 * par
    share = groups == 2 and hs % 2 == 0
    hh = hs // 2 if share else hs
    voff = grp * hh if share else 0
    hp = heads // QPARTS

    barrier = pltpu.get_barrier_semaphore()
    for k in range(1, n):
        pl.semaphore_signal(barrier, inc=1, device_id={"seq": lax.rem(me + k, n)}, device_id_type=MESH)
    pl.semaphore_signal(barrier, inc=1, device_id={"mp": 1 - half}, device_id_type=MESH)
    if share:
        pl.semaphore_signal(barrier, inc=1, device_id={"groups": 1 - grp}, device_id_type=MESH)

    loads = [pltpu.make_async_copy(a, b, lsem.at[i]) for i, (a, b) in enumerate((
        (qn_hbm, qn), (wuk_hbm, wuk), (lengths_hbm, lengths), (table_hbm, table), (qr_hbm, qr), (rope_hbm, rope)))]
    for copy in loads:
        copy.start()
    nb = bulk.shape[0] // 2
    step_l = slots // nb
    big = [pltpu.make_async_copy(lat_hbm.at[pl.ds(i * step_l, step_l)], lat.at[pl.ds(i * step_l, step_l)], bulk.at[i])
           for i in range(nb)]
    step_w = w_buf.shape[0] // nb
    bigw = [pltpu.make_async_copy(w_hbm.at[pl.ds(i * step_w, step_w)], w_buf.at[pl.ds(i * step_w, step_w)], bulk.at[nb + i])
            for i in range(nb)]
    own_v = pltpu.make_async_copy(v_hbm.at[pl.ds(me * hs, hs)], vbuf.at[me], lsem.at[6])

    def remote(src, dst, s, r, where):
        return pltpu.make_async_remote_copy(
            src_ref=src, dst_ref=dst, send_sem=s, recv_sem=r, device_id=where, device_id_type=MESH)

    loads[0].wait()
    for b in range(seqs):
        flat[b * heads:(b + 1) * heads, :] = qn[b].astype(F32)
    loads[1].wait()
    for copy in big:
        copy.start()

    def q_copy(block, i, k, peer, s, r):
        return remote(gath.at[block, i], gath.at[block, i], s.at[i * line + k], r.at[i * line + k], {"seq": peer})

    along, across = [], []
    for i in range(QPARTS):
        for h in range(i * hp, (i + 1) * hp):
            q = flat[pl.ds(h, seqs, stride=heads), :].astype(BF16)
            raw[h * seqs:(h + 1) * seqs, :] = lax.dot_general(
                q, wuk[h], (((1,), (1,)), ((), ())), preferred_element_type=F32)
        for p in range(seqs // pack):
            parts = [raw[pl.ds(i * hp * seqs + p * pack + j, hp, stride=seqs), :] for j in range(pack)]
            whole = parts[0] if pack == 1 else jnp.concatenate(parts, axis=1)
            gath[me, i, p * hp:(p + 1) * hp, :] = whole.astype(BF16)
        if i == 0:
            pl.semaphore_wait(barrier, n - 1 + 1 + int(share))
        for k in range(1, line):
            copy = q_copy(me, i, k, lax.rem(me + 2 * k, n), qs1, qr1)
            copy.start()
            along.append((i, k, copy))
        copy = q_copy(me, i, 0, partner, qs2, qr2)
        copy.start()
        across.append(copy)

    loads[2].wait()
    loads[3].wait()
    make_plan((me * slots, slots), page, lengths, table, plan_v)
    plan_copy = pltpu.make_async_copy(plan_v, plan, lsem.at[7])
    plan_copy.start()
    loads[4].wait()
    loads[5].wait()
    own_v.start()
    per = page * 128 // rope.shape[1]
    lane = lax.broadcasted_iota(jnp.int32, (slots, 128), 1) // (128 // per)

    def widen(i):
        x = rope[:, i * 128:(i + 1) * 128].astype(F32)
        for j in range(per):
            wide_rope[pl.ds(i * per + j, slots, stride=page), :] = jnp.where(lane == j, x, 0.0)

    fillers = list(range(rope.shape[1] // 128))
    each = -(-len(fillers) // max(1, len(along)))
    for i, k, copy in along:
        for f in fillers[:each]:
            widen(f)
        fillers = fillers[each:]
        copy.wait_recv()
        forward = q_copy(lax.rem(me - 2 * k + n, n), i, k, partner, qs2, qr2)
        forward.start()
        across.append(forward)

    def v_copy(k):
        peer = lax.rem(me + k, n)
        return remote(v_hbm.at[pl.ds(peer * hs + voff, hh)], vbuf.at[me, pl.ds(voff, hh)], vs1.at[k], vr1.at[k],
                      {"seq": peer})

    def twin_copy(k):
        s = lax.rem(me - k + n, n)
        return remote(vbuf.at[s, pl.ds(voff, hh)], vbuf.at[s, pl.ds(voff, hh)], vs2.at[k], vr2.at[k],
                      {"groups": 1 - grp})

    for k in range(2, n, 2):
        v_copy(k).start()

    def narrow(i, _):
        spread[i] = wide_rope[pl.ds(pl.multiple_of(i * page, page), page), :].astype(BF16)
        return 0

    lax.fori_loop(0, slots, narrow, 0, unroll=4)
    for b in range(seqs):
        turn[b] = jnp.concatenate([qr[b]] * (128 // qr.shape[2]), axis=1)
    run[0] = jnp.zeros(run.shape[1:], F32)
    tops[0] = jnp.full(tops.shape[1:], NEG, F32)
    sums[0] = jnp.zeros(sums.shape[1:], F32)
    plan_copy.wait()
    for copy in big:
        copy.wait()
    for copy in bigw:
        copy.start()
    for i, k, copy in along:
        copy.wait_send()
    for copy in across:
        copy.wait()
    for k in range(1, n, 2):
        v_copy(k).start()
    for i in range(QPARTS):
        for s in range(n):
            for b in range(seqs):
                at = b % pack * cols
                q_all[b, i * hp:(i + 1) * hp, s * cols:(s + 1) * cols] = gath[
                    s, i, b // pack * hp:(b // pack + 1) * hp, at:at + cols]

    tokens = GROUP * page
    tlane = lax.broadcasted_iota(jnp.int32, (1, tokens), 1)
    nt = (((1,), (1,)), ((), ()))

    def keys_of(c):
        return jnp.concatenate([lat[plan[0, c * GROUP + g]] for g in range(GROUP)], axis=0)

    def score_of(c):
        b = plan[2, c]
        turned = jnp.concatenate([spread[plan[0, c * GROUP + g]] for g in range(GROUP)], axis=0)
        limit = jnp.zeros((1, tokens), jnp.int32)
        for g in range(GROUP):
            limit = jnp.where(tlane // page == g, plan[1, c * GROUP + g] + g * page, limit)
        score = lax.dot_general(turn[b], turned, nt, preferred_element_type=F32)
        score = (score + lax.dot_general(q_all[b], keys_of(c), nt, preferred_element_type=F32)) * scale
        return jnp.where(tlane < limit, score, NEG)

    for u in range(UNROLL):
        ready[u] = score_of(u)

    def step(it, _):
        first = it * UNROLL
        scores = [ready[u] for u in range(UNROLL)]
        upcoming = [score_of(first + UNROLL + u) for u in range(UNROLL)]
        top, total, acc = tops[first][:, :1], sums[first][:, :1], run[first]
        for u in range(UNROLL):
            c = first + u
            old = jnp.where(plan[3, c] > 0, NEG, top)
            top = jnp.maximum(old, jnp.max(scores[u], axis=1, keepdims=True))
            weight = jnp.exp(scores[u] - top)
            carry = jnp.exp(old - top)
            product = jnp.dot(weight.astype(BF16), keys_of(c), preferred_element_type=F32)
            total = total * carry + jnp.sum(weight, axis=1, keepdims=True)
            acc = acc * carry + product
            tops[c + 1] = jnp.broadcast_to(top, tops.shape[1:])
            sums[c + 1] = jnp.broadcast_to(total, sums.shape[1:])
            run[c + 1] = acc
        for u in range(UNROLL):
            ready[u] = upcoming[u]
        return 0

    trips = nch // UNROLL
    relays = list(range(2, n, 2)) if share else []
    done = 0
    if relays:
        lead = trips - trips // 5 * len(relays)
        stride = trips // 5
        lax.fori_loop(0, lead, step, 0)

        def segment(j, _):
            v_copy(2 * j + 2).wait_recv()
            twin_copy(2 * j + 2).start()
            lax.fori_loop(lead + j * stride, lead + (j + 1) * stride, step, 0)
            return 0

        lax.fori_loop(0, len(relays), segment, 0)
    else:
        lax.fori_loop(0, trips, step, 0)

    ids = lax.broadcasted_iota(jnp.int32, (heads, 128), 1)
    all_top = jnp.full((heads, 128), NEG, F32)
    all_sum = jnp.zeros((heads, 128), F32)
    for p in range(seqs // 2):
        pair = []
        for b in (2 * p, 2 * p + 1):
            entry = plan[4, b]
            bt, bs = tops[entry], sums[entry]
            all_top = jnp.where(ids == b, bt, all_top)
            all_sum = jnp.where(ids == b, bs, all_sum)
            pair.append(run[entry] * (1.0 / jnp.maximum(bs[:, :1], 1e-30)))
        for d in range(n):
            mix[d, 2 * p * hs:2 * (p + 1) * hs, :] = jnp.concatenate(
                [x[d * hs:(d + 1) * hs] for x in pair], axis=0).astype(BF16)
    for d in range(n):
        st[d, :hs, :] = all_top[d * hs:(d + 1) * hs]
        st[d, hs:, :] = all_sum[d * hs:(d + 1) * hs]

    order = list(range(1, line)) + [0]
    sent = []
    for k in order:
        r = lax.rem(row + k, line)
        d = 2 * r + 1 - par
        for src, dst, s, rr in ((st, yst, yss, ysr), (mix, ygot, ys, yr)):
            copy = remote(src.at[d], dst.at[r], s.at[k], rr.at[k], {"seq": partner})
            copy.start()
            sent.append(copy)
    if share:
        for k in (1, 3):
            v_copy(k).wait_recv()
            twin_copy(k).start()
    onward = []
    for i, k in enumerate(order):
        sent[2 * i].wait_recv()
        sent[2 * i + 1].wait_recv()
        r = lax.rem(row + k, line)
        mine = 2 * r + par
        o, best, total = merge(seqs, [st[mine], yst[r]], [mix[mine].astype(F32), ygot[r].astype(F32)])
        zst[k, :hs, :] = best
        zst[k, hs:, :] = total
        zout[k] = o.astype(BF16)
        if k:
            for src, dst, s, rr in ((zst, zgst, zss, zsr), (zout, zgot, zs, zr)):
                copy = remote(src.at[k], dst.at[k], s.at[k], rr.at[k], {"seq": lax.rem(me + 2 * k, n)})
                copy.start()
                onward.append(copy)
    if share:
        for k in range(5, n, 2):
            v_copy(k).wait_recv()
            twin_copy(k).start()
    for copy in onward:
        copy.wait_recv()
    o, _, _ = merge(seqs, [zst[0]] + [zgst[k] for k in range(1, line)],
                    [zout[0].astype(F32)] + [zgot[k].astype(F32) for k in range(1, line)])
    blocks = width // 128
    for j in range(blocks):
        port[j] = o[:, j * 128:(j + 1) * 128]

    own_v.wait()
    for k in range(1, n):
        if share:
            twin_copy(k).wait_recv()
        else:
            v_copy(k).wait_recv()
    vdim = vbuf.shape[3]
    for h in range(hs):
        x = jnp.concatenate([port[j, pl.ds(h, seqs, stride=hs), :] for j in range(blocks)], axis=1).astype(BF16)
        wv = vbuf[:, h].reshape(width, vdim)
        vals[me, :, h * vdim:(h + 1) * vdim] = jnp.dot(x, wv, preferred_element_type=F32).astype(BF16)
    copies = []
    for k in range(1, n):
        copy = remote(vals.at[me], vals.at[me], as_.at[k], ar.at[k], {"seq": lax.rem(me + k, n)})
        copy.start()
        copies.append(copy)
    for copy in bigw:
        copy.wait()
    rows = hs * vdim
    res = None
    for k in range(n):
        src = lax.rem(me - k + n, n)
        if k:
            copies[k - 1].wait_recv()
        at = pl.ds(pl.multiple_of(src * rows, rows), rows)
        product = jnp.dot(vals[src], w_buf[at, :], preferred_element_type=F32)
        res = product if res is None else res + product
    wide = res.shape[1] // 2
    low, high = res[:, :wide], res[:, wide:]
    first = half == 0
    tx[...] = jnp.where(first, high, low)
    copy = remote(tx, rx, ms, mr, {"mp": 1 - half})
    copy.start()
    for c in copies + sent + onward:
        c.wait_send()
    for k in range(1, n):
        v_copy(k).wait_send()
        if share:
            twin_copy(k).wait_send()
    copy.wait()
    out_ref[...] = (jnp.where(first, low, high) + rx[...]).astype(BF16)


def local(n, groups, latent_cache, rope_cache, q_nope, q_rope, w_uk, value_up_weight, w_out, page_table, lengths):
    slots, page, width = latent_cache.shape
    seqs, heads, nope = q_nope.shape
    rope_w = q_rope.shape[2]
    cols = w_uk.shape[2]
    vdim = value_up_weight.shape[2]
    scale = (nope + rope_w) ** (-0.5)
    pack = max(1, min(seqs, 128 // cols))
    lanes = pack * cols
    hs = heads // n
    line = n // 2
    rows = seqs * hs
    wide = w_out.shape[1]
    nch = (slots + seqs * (GROUP - 1)) // GROUP
    nch = -(-nch // UNROLL) * UNROLL
    pw = ((nch + UNROLL) * GROUP + 127) // 128 * 128
    vm = pl.BlockSpec(memory_space=pltpu.VMEM)
    hbm = pl.BlockSpec(memory_space=pl.ANY)
    dma = pltpu.SemaphoreType.DMA
    vmem = pltpu.VMEM
    bulk = 8
    return pl.pallas_call(
        functools.partial(kernel, n, groups, pack, scale, nch),
        out_shape=jax.ShapeDtypeStruct((seqs, wide // 2), BF16),
        in_specs=[hbm] * 9, out_specs=vm,
        scratch_shapes=[
            pltpu.SMEM(lengths.shape, jnp.int32),
            vmem(page_table.shape, jnp.int32),
            vmem(rope_cache.shape, BF16),
            vmem(q_nope.shape, BF16),
            vmem((heads, cols, nope), BF16),
            vmem(q_rope.shape, BF16),
            vmem(latent_cache.shape, BF16),
            vmem(w_out.shape, BF16),
            vmem((8, pw), jnp.int32),
            pltpu.SMEM((8, pw), jnp.int32),
            vmem((heads * seqs, cols), F32),
            vmem((heads * seqs, nope), F32),
            vmem((n, QPARTS, seqs // pack * heads // QPARTS, lanes), BF16),
            vmem((seqs, heads, width), BF16),
            vmem((seqs, heads, 128), BF16),
            vmem((slots * page, 128), F32),
            vmem((slots, page, 128), BF16),
            vmem((nch + 1, heads, width), F32),
            vmem((nch + 1, heads, 128), F32),
            vmem((nch + 1, heads, 128), F32),
            vmem((UNROLL, heads, GROUP * page), F32),
            vmem((n, rows, width), BF16),
            vmem((n, 2 * hs, 128), F32),
            vmem((line, rows, width), BF16),
            vmem((line, 2 * hs, 128), F32),
            vmem((line, rows, width), BF16),
            vmem((line, 2 * hs, 128), F32),
            vmem((line, rows, width), BF16),
            vmem((line, 2 * hs, 128), F32),
            vmem((width // 128, rows, 128), F32),
            vmem((n, hs, cols, vdim), BF16),
            vmem((n, seqs, hs * vdim), BF16),
            vmem((seqs, wide // 2), F32),
            vmem((seqs, wide // 2), F32),
            dma((8,)), dma((2 * bulk,)),
            dma((QPARTS * line,)), dma((QPARTS * line,)), dma((QPARTS * line,)), dma((QPARTS * line,)),
            dma((n,)), dma((n,)), dma((n,)), dma((n,)),
            dma((line,)), dma((line,)), dma((line,)), dma((line,)),
            dma((line,)), dma((line,)), dma((line,)), dma((line,)),
            dma((n,)), dma((n,)), dma, dma,
        ],
        compiler_params=pltpu.CompilerParams(
            has_side_effects=True, collective_id=1, vmem_limit_bytes=60 * 1024 * 1024),
        name="decode",
    )(lengths, page_table, rope_cache, q_nope, w_uk.transpose(0, 2, 1), q_rope, latent_cache, value_up_weight, w_out)


def solution(mesh):
    return jax.shard_map(
        functools.partial(local, mesh.shape["seq"], mesh.shape["groups"]),
        mesh=mesh,
        in_specs=(
            P(("groups", "seq"), None, None),
            P(("groups", "seq"), None),
            P("groups", "mp", None),
            P("groups", "mp", None),
            P("mp", None, "seq"),
            P("mp", "seq", None),
            P("mp", "seq"),
            P("groups", None),
            P("groups"),
        ),
        out_specs=P("groups", ("seq", "mp")),
        check_vma=False,
    )
```

time: 69.9 us -> 49 us (0.70)
  Pallas kernels: 68.7 us -> 47.5 us
    pallas_call x3 -> x1, Pallas kernels: 68.7 us -> 47.5 us  [local(): pl.pallas_call(functools.partial(kernel, n, groups, pack, scale, nch), ou...]
where the time goes in v1:
time: 49 us; the launch traced here: 48.8 us
  Pallas kernels  47.5 us (97%)
  local copies, waits for them, and re-layouts  1.3 us (3%)
    pallas_call x1, Pallas kernels, local(): pl.pallas_call(functools.partial(kernel, n, groups, pack, scale, nch), ou...  47.5 us
    unnamed x1, local copies, waits for them, and re-layouts  1.3 us

profile of v1, /device:TPU:0, one launch (start us, length us, event | category | flops | bytes accessed | tf_op | source)
XLA Modules:
  0.0 48.8 jit_solution(14099045975535999508)
XLA Ops:
  0.0 47.5 %decode.1 = bf16[8,448]{1,0:T(8,128)(2,1)} custom-call(s32[8]{0:T(128)} %lengths_hbm.1, s32[8,256]{1,0:T(8,128)} %table_hbm.1, bf16[128,4096]{1,0:T(8,128)(2,1)} %rope_hbm.1, bf16[8,64,128]{2,1,0:T(8,128)(2,1)} %qn_hbm.1, bf16[64,64,128]{2,1,0:T(8,128)(2,1)} %bitcast.1, bf16[8,64,64]{2,1,0:T(8,128)(2,1)} %qr_hbm.1, bf16[128,64,512]{2,1,0:T(8,128)(2,1)} %lat_hbm.1, ...), custom_call_target="tpu_custom_call" | custom-call | tf_op jit(solution)/shard_map/decode/pallas_call | solution.py:404
  47.5 1.3 %copy.11 = bf16[8,448]{1,0:T(8,128)(2,1)} copy(bf16[8,448]{1,0:T(8,128)(2,1)} %decode.1) | data formatting | bytes 14336

commit v2 on v1

--- a/solution.py
+++ b/solution.py
@@ -1,4 +1,5 @@
 import functools
+import math
 
 import jax
 import jax.numpy as jnp
@@ -10,7 +11,7 @@
 NEG = -1e30
 MESH = pl.DeviceIdType.MESH
 GROUP = 4
-UNROLL = 2
+UNROLL = 10
 QPARTS = 2
 F32 = jnp.float32
 BF16 = jnp.bfloat16
@@ -64,7 +65,7 @@
     hs = stats[0].shape[0] // 2
     tops = [s[:hs] for s in stats]
     best = functools.reduce(jnp.maximum, tops)
-    shares = [s[hs:] * jnp.exp(t - best) for s, t in zip(stats, tops)]
+    shares = [s[hs:] * jnp.exp2(t - best) for s, t in zip(stats, tops)]
     total = functools.reduce(jnp.add, shares)
     inv = 1.0 / jnp.maximum(total, 1e-30)
     out = None
@@ -78,8 +79,8 @@
 
 def kernel(n, groups, pack, scale, nch,
            lengths_hbm, table_hbm, rope_hbm, qn_hbm, wuk_hbm, qr_hbm, lat_hbm, v_hbm, w_hbm, out_ref,
-           lengths, table, rope, qn, wuk, qr, lat, w_buf, plan_v, plan, raw, flat, gath, q_all, turn,
-           wide_rope, spread, run, tops, sums, ready, mix, st, ygot, yst, zout, zst, zgot, zgst, port,
+           lengths, table, rope, qn, wuk, qr, lat, w_buf, plan_v, plan, raw, flat, gath, q_near, q_far, turn,
+           wide_rope, spread, run, tops, sums, peak, part, mix, st, ygot, yst, zout, zst, zgot, zgst, port,
            vbuf, vals, tx, rx,
            lsem, bulk, qs1, qr1, qs2, qr2, vs1, vr1, vs2, vr2, ys, yr, yss, ysr, zs, zr, zss, zsr, as_, ar, ms, mr):
     me = lax.axis_index("seq")
@@ -87,7 +88,8 @@
     grp = lax.axis_index("groups")
     seqs, heads, _ = qn.shape
     cols = wuk.shape[1]
-    slots, page, width = lat.shape
+    _, slots, page, wing = lat.shape
+    width = 2 * wing
     hs = heads // n
     line = n // 2
     par = lax.rem(me, 2)
@@ -97,6 +99,13 @@
     hh = hs // 2 if share else hs
     voff = grp * hh if share else 0
     hp = heads // QPARTS
+    near_n = line // 2
+    side, pos = row // near_n, lax.rem(row, near_n)
+
+    def along_of(j, sign):
+        other, k = (0, j) if j < near_n else (1, j - near_n)
+        at = lax.rem(pos + sign * k + near_n, near_n)
+        return 2 * ((side + other * (1 - 2 * side)) * near_n + at) + par
 
     barrier = pltpu.get_barrier_semaphore()
     for k in range(1, n):
@@ -110,9 +119,10 @@
     for copy in loads:
         copy.start()
     nb = bulk.shape[0] // 2
-    step_l = slots // nb
-    big = [pltpu.make_async_copy(lat_hbm.at[pl.ds(i * step_l, step_l)], lat.at[pl.ds(i * step_l, step_l)], bulk.at[i])
-           for i in range(nb)]
+    step_l = 2 * slots // nb
+    big = [pltpu.make_async_copy(
+        lat_hbm.at[pl.ds(i // 2 * step_l, step_l), :, pl.ds(i % 2 * wing, wing)],
+        lat.at[i % 2, pl.ds(i // 2 * step_l, step_l)], bulk.at[i]) for i in range(nb)]
     step_w = w_buf.shape[0] // nb
     bigw = [pltpu.make_async_copy(w_hbm.at[pl.ds(i * step_w, step_w)], w_buf.at[pl.ds(i * step_w, step_w)], bulk.at[nb + i])
             for i in range(nb)]
@@ -145,12 +155,22 @@
         if i == 0:
             pl.semaphore_wait(barrier, n - 1 + 1 + int(share))
         for k in range(1, line):
-            copy = q_copy(me, i, k, lax.rem(me + 2 * k, n), qs1, qr1)
+            copy = q_copy(me, i, k, along_of(k, 1), qs1, qr1)
             copy.start()
             along.append((i, k, copy))
         copy = q_copy(me, i, 0, partner, qs2, qr2)
         copy.start()
-        across.append(copy)
+        across.append((0, copy))
+
+    def v_copy(k):
+        peer = lax.rem(me + k, n)
+        return remote(v_hbm.at[pl.ds(peer * hs + voff, hh)], vbuf.at[me, pl.ds(voff, hh)], vs1.at[k], vr1.at[k],
+                      {"seq": peer})
+
+    def twin_copy(k):
+        s = lax.rem(me - k + n, n)
+        return remote(vbuf.at[s, pl.ds(voff, hh)], vbuf.at[s, pl.ds(voff, hh)], vs2.at[k], vr2.at[k],
+                      {"groups": 1 - grp})
 
     loads[2].wait()
     loads[3].wait()
@@ -161,42 +181,36 @@
     loads[5].wait()
     own_v.start()
     per = page * 128 // rope.shape[1]
+    pitch = wide_rope.shape[0] // slots
     lane = lax.broadcasted_iota(jnp.int32, (slots, 128), 1) // (128 // per)
 
     def widen(i):
         x = rope[:, i * 128:(i + 1) * 128].astype(F32)
         for j in range(per):
-            wide_rope[pl.ds(i * per + j, slots, stride=page), :] = jnp.where(lane == j, x, 0.0)
-
-    fillers = list(range(rope.shape[1] // 128))
-    each = -(-len(fillers) // max(1, len(along)))
-    for i, k, copy in along:
-        for f in fillers[:each]:
+            wide_rope[pl.ds(i * per + j, slots, stride=pitch), :] = jnp.where(lane == j, x, 0.0)
+
+    def narrow(i, _):
+        spread[i] = wide_rope[pl.ds(pl.multiple_of(i * pitch, 8), page), :].astype(BF16)
+        return 0
+
+    along.sort(key=lambda x: (x[1] >= near_n, x[0], x[1]))
+    steps = rope.shape[1] // 128
+    share_w = -(-steps // max(1, len(along) // 2))
+    for i, (q, k, copy) in enumerate(along):
+        for f in range(min(steps, i * share_w), min(steps, (i + 1) * share_w)):
             widen(f)
-        fillers = fillers[each:]
+        if (i + 1) * share_w >= steps > i * share_w:
+            lax.fori_loop(0, slots, narrow, 0, unroll=4)
         copy.wait_recv()
-        forward = q_copy(lax.rem(me - 2 * k + n, n), i, k, partner, qs2, qr2)
+        forward = q_copy(along_of(k, -1), q, k, partner, qs2, qr2)
         forward.start()
-        across.append(forward)
-
-    def v_copy(k):
-        peer = lax.rem(me + k, n)
-        return remote(v_hbm.at[pl.ds(peer * hs + voff, hh)], vbuf.at[me, pl.ds(voff, hh)], vs1.at[k], vr1.at[k],
-                      {"seq": peer})
-
-    def twin_copy(k):
-        s = lax.rem(me - k + n, n)
-        return remote(vbuf.at[s, pl.ds(voff, hh)], vbuf.at[s, pl.ds(voff, hh)], vs2.at[k], vr2.at[k],
-                      {"groups": 1 - grp})
+        across.append((k, forward))
 
     for k in range(2, n, 2):
         v_copy(k).start()
-
-    def narrow(i, _):
-        spread[i] = wide_rope[pl.ds(pl.multiple_of(i * page, page), page), :].astype(BF16)
-        return 0
-
-    lax.fori_loop(0, slots, narrow, 0, unroll=4)
+    for k in range(1, n, 2):
+        v_copy(k).start()
+
     for b in range(seqs):
         turn[b] = jnp.concatenate([qr[b]] * (128 // qr.shape[2]), axis=1)
     run[0] = jnp.zeros(run.shape[1:], F32)
@@ -207,78 +221,84 @@
         copy.wait()
     for copy in bigw:
         copy.start()
-    for i, k, copy in along:
-        copy.wait_send()
-    for copy in across:
-        copy.wait()
-    for k in range(1, n, 2):
-        v_copy(k).start()
-    for i in range(QPARTS):
-        for s in range(n):
-            for b in range(seqs):
-                at = b % pack * cols
-                q_all[b, i * hp:(i + 1) * hp, s * cols:(s + 1) * cols] = gath[
-                    s, i, b // pack * hp:(b // pack + 1) * hp, at:at + cols]
+
+    def assemble(first, dst):
+        for i in range(QPARTS):
+            for s in range(n // 2):
+                for b in range(seqs):
+                    at = b % pack * cols
+                    dst[b, i * hp:(i + 1) * hp, s * cols:(s + 1) * cols] = gath[
+                        first + s, i, b // pack * hp:(b // pack + 1) * hp, at:at + cols]
 
     tokens = GROUP * page
     tlane = lax.broadcasted_iota(jnp.int32, (1, tokens), 1)
     nt = (((1,), (1,)), ((), ()))
 
-    def keys_of(c):
-        return jnp.concatenate([lat[plan[0, c * GROUP + g]] for g in range(GROUP)], axis=0)
-
-    def score_of(c):
-        b = plan[2, c]
-        turned = jnp.concatenate([spread[plan[0, c * GROUP + g]] for g in range(GROUP)], axis=0)
-        limit = jnp.zeros((1, tokens), jnp.int32)
-        for g in range(GROUP):
-            limit = jnp.where(tlane // page == g, plan[1, c * GROUP + g] + g * page, limit)
-        score = lax.dot_general(turn[b], turned, nt, preferred_element_type=F32)
-        score = (score + lax.dot_general(q_all[b], keys_of(c), nt, preferred_element_type=F32)) * scale
-        return jnp.where(tlane < limit, score, NEG)
-
-    for u in range(UNROLL):
-        ready[u] = score_of(u)
-
-    def step(it, _):
-        first = it * UNROLL
-        scores = [ready[u] for u in range(UNROLL)]
-        upcoming = [score_of(first + UNROLL + u) for u in range(UNROLL)]
-        top, total, acc = tops[first][:, :1], sums[first][:, :1], run[first]
+    def slots_of(ref, c):
+        return jnp.concatenate([ref[plan[0, c * GROUP + g]] for g in range(GROUP)], axis=0)
+
+    def first_pass(it, _):
         for u in range(UNROLL):
-            c = first + u
-            old = jnp.where(plan[3, c] > 0, NEG, top)
-            top = jnp.maximum(old, jnp.max(scores[u], axis=1, keepdims=True))
-            weight = jnp.exp(scores[u] - top)
-            carry = jnp.exp(old - top)
-            product = jnp.dot(weight.astype(BF16), keys_of(c), preferred_element_type=F32)
-            total = total * carry + jnp.sum(weight, axis=1, keepdims=True)
-            acc = acc * carry + product
-            tops[c + 1] = jnp.broadcast_to(top, tops.shape[1:])
-            sums[c + 1] = jnp.broadcast_to(total, sums.shape[1:])
+            c = it * UNROLL + u
+            b = plan[2, c]
+            limit = jnp.zeros((1, tokens), jnp.int32)
+            for g in range(GROUP):
+                limit = jnp.where(tlane // page == g, plan[1, c * GROUP + g] + g * page, limit)
+            score = lax.dot_general(turn[b], slots_of(spread, c), nt, preferred_element_type=F32)
+            score = score + lax.dot_general(q_near[b], slots_of(lat.at[side], c), nt, preferred_element_type=F32)
+            part[c] = jnp.where(tlane < limit, score, NEG)
+        return 0
+
+    for k, copy in across:
+        if k < near_n:
+            copy.wait_recv()
+    assemble(side * (n // 2), q_near)
+    trips = nch // UNROLL
+    lax.fori_loop(0, trips, first_pass, 0)
+    for k, copy in across:
+        if k >= near_n:
+            copy.wait_recv()
+    assemble((1 - side) * (n // 2), q_far)
+
+    def second_pass(it, _):
+        top = tops[it * UNROLL]
+        for u in range(UNROLL):
+            c = it * UNROLL + u
+            far = lax.dot_general(q_far[plan[2, c]], slots_of(lat.at[1 - side], c), nt, preferred_element_type=F32)
+            score = (part[c] + far) * scale
+            part[c] = score
+            top = jnp.where(plan[3, c] > 0, NEG, top)
+            for j in range(tokens // 128):
+                top = jnp.maximum(top, score[:, j * 128:(j + 1) * 128])
+            tops[c + 1] = top
+        return 0
+
+    lax.fori_loop(0, trips, second_pass, 0)
+    for b in range(seqs):
+        peak[b] = jnp.broadcast_to(jnp.max(tops[plan[4, b]], axis=1, keepdims=True), peak.shape[1:])
+
+    def third_pass(it, _):
+        acc, total = run[it * UNROLL], sums[it * UNROLL]
+        for u in range(UNROLL):
+            c = it * UNROLL + u
+            top = peak[plan[2, c]]
+            keep = jnp.where(plan[3, c] > 0, 0.0, 1.0)
+            weight = [jnp.exp2(part[c, :, j * 128:(j + 1) * 128] - top) for j in range(tokens // 128)]
+            total = total * keep + functools.reduce(jnp.add, weight)
+            weight = jnp.concatenate([x.astype(BF16) for x in weight], axis=1)
+            product = jnp.concatenate(
+                [jnp.dot(weight, slots_of(lat.at[j], c), preferred_element_type=F32) for j in range(2)], axis=1)
+            acc = acc * keep + product
+            sums[c + 1] = total
             run[c + 1] = acc
-        for u in range(UNROLL):
-            ready[u] = upcoming[u]
         return 0
 
-    trips = nch // UNROLL
-    relays = list(range(2, n, 2)) if share else []
-    done = 0
-    if relays:
-        lead = trips - trips // 5 * len(relays)
-        stride = trips // 5
-        lax.fori_loop(0, lead, step, 0)
-
-        def segment(j, _):
-            v_copy(2 * j + 2).wait_recv()
-            twin_copy(2 * j + 2).start()
-            lax.fori_loop(lead + j * stride, lead + (j + 1) * stride, step, 0)
-            return 0
-
-        lax.fori_loop(0, len(relays), segment, 0)
-    else:
-        lax.fori_loop(0, trips, step, 0)
-
+    lax.fori_loop(0, trips, third_pass, 0)
+
+    if share:
+        for k in range(2, n, 2):
+            v_copy(k).wait_recv()
+            twin_copy(k).start()
     ids = lax.broadcasted_iota(jnp.int32, (heads, 128), 1)
     all_top = jnp.full((heads, 128), NEG, F32)
     all_sum = jnp.zeros((heads, 128), F32)
@@ -286,10 +306,10 @@
         pair = []
         for b in (2 * p, 2 * p + 1):
             entry = plan[4, b]
-            bt, bs = tops[entry], sums[entry]
-            all_top = jnp.where(ids == b, bt, all_top)
-            all_sum = jnp.where(ids == b, bs, all_sum)
-            pair.append(run[entry] * (1.0 / jnp.maximum(bs[:, :1], 1e-30)))
+            total = jnp.sum(sums[entry], axis=1, keepdims=True)
+            all_top = jnp.where(ids == b, peak[b], all_top)
+            all_sum = jnp.where(ids == b, total, all_sum)
+            pair.append(run[entry] * (1.0 / jnp.maximum(total, 1e-30)))
         for d in range(n):
             mix[d, 2 * p * hs:2 * (p + 1) * hs, :] = jnp.concatenate(
                 [x[d * hs:(d + 1) * hs] for x in pair], axis=0).astype(BF16)
@@ -370,7 +390,7 @@
     tx[...] = jnp.where(first, high, low)
     copy = remote(tx, rx, ms, mr, {"mp": 1 - half})
     copy.start()
-    for c in copies + sent + onward:
+    for c in copies + sent + onward + [x[2] for x in along] + [x[1] for x in across]:
         c.wait_send()
     for k in range(1, n):
         v_copy(k).wait_send()
@@ -386,7 +406,7 @@
     rope_w = q_rope.shape[2]
     cols = w_uk.shape[2]
     vdim = value_up_weight.shape[2]
-    scale = (nope + rope_w) ** (-0.5)
+    scale = (nope + rope_w) ** (-0.5) * math.log2(math.e)
     pack = max(1, min(seqs, 128 // cols))
     lanes = pack * cols
     hs = heads // n
@@ -395,7 +415,7 @@
     wide = w_out.shape[1]
     nch = (slots + seqs * (GROUP - 1)) // GROUP
     nch = -(-nch // UNROLL) * UNROLL
-    pw = ((nch + UNROLL) * GROUP + 127) // 128 * 128
+    pw = (nch * GROUP + 127) // 128 * 128
     vm = pl.BlockSpec(memory_space=pltpu.VMEM)
     hbm = pl.BlockSpec(memory_space=pl.ANY)
     dma = pltpu.SemaphoreType.DMA
@@ -412,21 +432,23 @@
             vmem(q_nope.shape, BF16),
             vmem((heads, cols, nope), BF16),
             vmem(q_rope.shape, BF16),
-            vmem(latent_cache.shape, BF16),
+            vmem((2, slots, page, width // 2), BF16),
             vmem(w_out.shape, BF16),
             vmem((8, pw), jnp.int32),
             pltpu.SMEM((8, pw), jnp.int32),
             vmem((heads * seqs, cols), F32),
             vmem((heads * seqs, nope), F32),
             vmem((n, QPARTS, seqs // pack * heads // QPARTS, lanes), BF16),
-            vmem((seqs, heads, width), BF16),
+            vmem((seqs, heads, width // 2), BF16),
+            vmem((seqs, heads, width // 2), BF16),
             vmem((seqs, heads, 128), BF16),
-            vmem((slots * page, 128), F32),
+            vmem((slots * (page + 8), 128), F32),
             vmem((slots, page, 128), BF16),
             vmem((nch + 1, heads, width), F32),
             vmem((nch + 1, heads, 128), F32),
             vmem((nch + 1, heads, 128), F32),
-            vmem((UNROLL, heads, GROUP * page), F32),
+            vmem((seqs, heads, 128), F32),
+            vmem((nch, heads, GROUP * page), F32),
             vmem((n, rows, width), BF16),
             vmem((n, 2 * hs, 128), F32),
             vmem((line, rows, width), BF16),

time: 49 us -> 46.1 us (0.941)
  Pallas kernels: 47.5 us -> 44.6 us
    pallas_call x1, Pallas kernels: 47.5 us -> 44.6 us  [local(): pl.pallas_call(functools.partial(kernel, n, groups, pack, scale, nch), ou...]
where the time goes in v2:
time: 46.1 us; the launch traced here: 45.9 us
  Pallas kernels  44.6 us (97%)
  local copies, waits for them, and re-layouts  1.3 us (3%)
    pallas_call x1, Pallas kernels, local(): pl.pallas_call(functools.partial(kernel, n, groups, pack, scale, nch), ou...  44.6 us
    unnamed x1, local copies, waits for them, and re-layouts  1.3 us

profile of v2, /device:TPU:0, one launch (start us, length us, event | category | flops | bytes accessed | tf_op | source)
XLA Modules:
  0.0 45.9 jit_solution(3562984420769728474)
XLA Ops:
  0.0 44.6 %decode.1 = bf16[8,448]{1,0:T(8,128)(2,1)} custom-call(s32[8]{0:T(128)} %lengths_hbm.1, s32[8,256]{1,0:T(8,128)} %table_hbm.1, bf16[128,4096]{1,0:T(8,128)(2,1)} %rope_hbm.1, bf16[8,64,128]{2,1,0:T(8,128)(2,1)} %qn_hbm.1, bf16[64,64,128]{2,1,0:T(8,128)(2,1)} %bitcast.1, bf16[8,64,64]{2,1,0:T(8,128)(2,1)} %qr_hbm.1, bf16[128,64,512]{2,1,0:T(8,128)(2,1)} %lat_hbm.1, ...), custom_call_target="tpu_custom_call" | custom-call | tf_op jit(solution)/shard_map/decode/pallas_call | solution.py:424
  44.6 1.3 %copy.11 = bf16[8,448]{1,0:T(8,128)(2,1)} copy(bf16[8,448]{1,0:T(8,128)(2,1)} %decode.1) | data formatting | bytes 14336

commit v3 on v2

--- a/solution.py
+++ b/solution.py
@@ -11,7 +11,8 @@
 NEG = -1e30
 MESH = pl.DeviceIdType.MESH
 GROUP = 4
-UNROLL = 10
+UNROLL = 20
+UNROLL1 = 10
 QPARTS = 2
 F32 = jnp.float32
 BF16 = jnp.bfloat16
@@ -61,26 +62,28 @@
     plan_ref[5:8, :] = jnp.zeros((3, wide), jnp.int32)
 
 
-def merge(seqs, stats, parts):
+def weigh(seqs, stats):
     hs = stats[0].shape[0] // 2
     tops = [s[:hs] for s in stats]
     best = functools.reduce(jnp.maximum, tops)
     shares = [s[hs:] * jnp.exp2(t - best) for s, t in zip(stats, tops)]
     total = functools.reduce(jnp.add, shares)
     inv = 1.0 / jnp.maximum(total, 1e-30)
-    out = None
-    for share, part in zip(shares, parts):
+    columns = []
+    for share in shares:
         share = share * inv
-        column = jnp.concatenate([share[:, b:b + 1] for b in range(seqs)], axis=0)
-        term = part * column
-        out = term if out is None else out + term
-    return out, best, total
+        columns.append(jnp.concatenate([share[:, b:b + 1] for b in range(seqs)], axis=0))
+    return columns, best, total
+
+
+def mean(columns, parts):
+    return functools.reduce(jnp.add, [p.astype(F32) * c for c, p in zip(columns, parts)])
 
 
 def kernel(n, groups, pack, scale, nch,
            lengths_hbm, table_hbm, rope_hbm, qn_hbm, wuk_hbm, qr_hbm, lat_hbm, v_hbm, w_hbm, out_ref,
            lengths, table, rope, qn, wuk, qr, lat, w_buf, plan_v, plan, raw, flat, gath, q_near, q_far, turn,
-           wide_rope, spread, run, tops, sums, peak, part, mix, st, ygot, yst, zout, zst, zgot, zgst, port,
+           wide_rope, spread, run, tops, sums, peak, part, wts, mix, st, ygot, yst, zout, zst, zgot, zgst, port,
            vbuf, vals, tx, rx,
            lsem, bulk, qs1, qr1, qs2, qr2, vs1, vr1, vs2, vr2, ys, yr, yss, ysr, zs, zr, zss, zsr, as_, ar, ms, mr):
     me = lax.axis_index("seq")
@@ -107,6 +110,12 @@
         at = lax.rem(pos + sign * k + near_n, near_n)
         return 2 * ((side + other * (1 - 2 * side)) * near_n + at) + par
 
+    rows_out = []
+    for j in range(line - 1):
+        down = jnp.where(line - 1 - j > row, line - 1 - j, line - 2 - j)
+        rows_out.append(jnp.where(side == 0, down, jnp.where(row > j, j, j + 1)))
+    peers = [2 * r + par for r in rows_out] + [2 * r + 1 - par for r in rows_out] + [partner]
+
     barrier = pltpu.get_barrier_semaphore()
     for k in range(1, n):
         pl.semaphore_signal(barrier, inc=1, device_id={"seq": lax.rem(me + k, n)}, device_id_type=MESH)
@@ -115,9 +124,10 @@
         pl.semaphore_signal(barrier, inc=1, device_id={"groups": 1 - grp}, device_id_type=MESH)
 
     loads = [pltpu.make_async_copy(a, b, lsem.at[i]) for i, (a, b) in enumerate((
-        (qn_hbm, qn), (wuk_hbm, wuk), (lengths_hbm, lengths), (table_hbm, table), (qr_hbm, qr), (rope_hbm, rope)))]
-    for copy in loads:
-        copy.start()
+        (qn_hbm, qn), (wuk_hbm.at[pl.ds(0, hp)], wuk.at[pl.ds(0, hp)]), (lengths_hbm, lengths), (table_hbm, table), (qr_hbm, qr), (rope_hbm, rope)) + tuple(
+            (wuk_hbm.at[pl.ds(i * hp, hp)], wuk.at[pl.ds(i * hp, hp)]) for i in range(1, QPARTS)))]
+    for i in (0, 1, *range(6, len(loads)), 2, 3, 4, 5):
+        loads[i].start()
     nb = bulk.shape[0] // 2
     step_l = 2 * slots // nb
     big = [pltpu.make_async_copy(
@@ -126,7 +136,7 @@
     step_w = w_buf.shape[0] // nb
     bigw = [pltpu.make_async_copy(w_hbm.at[pl.ds(i * step_w, step_w)], w_buf.at[pl.ds(i * step_w, step_w)], bulk.at[nb + i])
             for i in range(nb)]
-    own_v = pltpu.make_async_copy(v_hbm.at[pl.ds(me * hs, hs)], vbuf.at[me], lsem.at[6])
+    own_v = pltpu.make_async_copy(v_hbm.at[pl.ds(me * hs, hs)], vbuf.at[me], lsem.at[5 + QPARTS])
 
     def remote(src, dst, s, r, where):
         return pltpu.make_async_remote_copy(
@@ -135,15 +145,16 @@
     loads[0].wait()
     for b in range(seqs):
         flat[b * heads:(b + 1) * heads, :] = qn[b].astype(F32)
-    loads[1].wait()
-    for copy in big:
-        copy.start()
 
     def q_copy(block, i, k, peer, s, r):
         return remote(gath.at[block, i], gath.at[block, i], s.at[i * line + k], r.at[i * line + k], {"seq": peer})
 
     along, across = [], []
     for i in range(QPARTS):
+        loads[5 + i if i else 1].wait()
+        if i == QPARTS - 1:
+            for copy in big:
+                copy.start()
         for h in range(i * hp, (i + 1) * hp):
             q = flat[pl.ds(h, seqs, stride=heads), :].astype(BF16)
             raw[h * seqs:(h + 1) * seqs, :] = lax.dot_general(
@@ -162,20 +173,21 @@
         copy.start()
         across.append((0, copy))
 
-    def v_copy(k):
-        peer = lax.rem(me + k, n)
-        return remote(v_hbm.at[pl.ds(peer * hs + voff, hh)], vbuf.at[me, pl.ds(voff, hh)], vs1.at[k], vr1.at[k],
-                      {"seq": peer})
-
-    def twin_copy(k):
-        s = lax.rem(me - k + n, n)
-        return remote(vbuf.at[s, pl.ds(voff, hh)], vbuf.at[s, pl.ds(voff, hh)], vs2.at[k], vr2.at[k],
-                      {"groups": 1 - grp})
+    def v_copy(d, s):
+        return remote(v_hbm.at[pl.ds(d * hs + voff, hh)], vbuf.at[s, pl.ds(voff, hh)], vs1.at[d], vr1.at[s], {"seq": d})
+
+    def twin_copy(s):
+        return remote(vbuf.at[s, pl.ds(voff, hh)], vbuf.at[s, pl.ds(voff, hh)], vs2.at[s], vr2.at[s], {"groups": 1 - grp})
+
+    def relay(sources):
+        for s in sources if share else []:
+            v_copy(s, s).wait_recv()
+            twin_copy(s).start()
 
     loads[2].wait()
     loads[3].wait()
     make_plan((me * slots, slots), page, lengths, table, plan_v)
-    plan_copy = pltpu.make_async_copy(plan_v, plan, lsem.at[7])
+    plan_copy = pltpu.make_async_copy(plan_v, plan, lsem.at[6 + QPARTS])
     plan_copy.start()
     loads[4].wait()
     loads[5].wait()
@@ -206,14 +218,13 @@
         forward.start()
         across.append((k, forward))
 
-    for k in range(2, n, 2):
-        v_copy(k).start()
-    for k in range(1, n, 2):
-        v_copy(k).start()
+    for d in peers:
+        v_copy(d, me).start()
 
     for b in range(seqs):
         turn[b] = jnp.concatenate([qr[b]] * (128 // qr.shape[2]), axis=1)
-    run[0] = jnp.zeros(run.shape[1:], F32)
+    for j in range(2):
+        run[j, 0] = jnp.zeros(run.shape[2:], F32)
     tops[0] = jnp.full(tops.shape[1:], NEG, F32)
     sums[0] = jnp.zeros(sums.shape[1:], F32)
     plan_copy.wait()
@@ -238,8 +249,8 @@
         return jnp.concatenate([ref[plan[0, c * GROUP + g]] for g in range(GROUP)], axis=0)
 
     def first_pass(it, _):
-        for u in range(UNROLL):
-            c = it * UNROLL + u
+        for u in range(UNROLL1):
+            c = it * UNROLL1 + u
             b = plan[2, c]
             limit = jnp.zeros((1, tokens), jnp.int32)
             for g in range(GROUP):
@@ -254,7 +265,7 @@
             copy.wait_recv()
     assemble(side * (n // 2), q_near)
     trips = nch // UNROLL
-    lax.fori_loop(0, trips, first_pass, 0)
+    lax.fori_loop(0, nch // UNROLL1, first_pass, 0)
     for k, copy in across:
         if k >= near_n:
             copy.wait_recv()
@@ -278,7 +289,7 @@
         peak[b] = jnp.broadcast_to(jnp.max(tops[plan[4, b]], axis=1, keepdims=True), peak.shape[1:])
 
     def third_pass(it, _):
-        acc, total = run[it * UNROLL], sums[it * UNROLL]
+        acc, total = run[0, it * UNROLL], sums[it * UNROLL]
         for u in range(UNROLL):
             c = it * UNROLL + u
             top = peak[plan[2, c]]
@@ -286,101 +297,118 @@
             weight = [jnp.exp2(part[c, :, j * 128:(j + 1) * 128] - top) for j in range(tokens // 128)]
             total = total * keep + functools.reduce(jnp.add, weight)
             weight = jnp.concatenate([x.astype(BF16) for x in weight], axis=1)
-            product = jnp.concatenate(
-                [jnp.dot(weight, slots_of(lat.at[j], c), preferred_element_type=F32) for j in range(2)], axis=1)
-            acc = acc * keep + product
+            wts[c] = weight
+            acc = acc * keep + jnp.dot(weight, slots_of(lat.at[0], c), preferred_element_type=F32)
             sums[c + 1] = total
-            run[c + 1] = acc
+            run[0, c + 1] = acc
         return 0
 
+    def fourth_pass(it, _):
+        acc = run[1, it * UNROLL]
+        for u in range(UNROLL):
+            c = it * UNROLL + u
+            keep = jnp.where(plan[3, c] > 0, 0.0, 1.0)
+            acc = acc * keep + jnp.dot(wts[c], slots_of(lat.at[1], c), preferred_element_type=F32)
+            run[1, c + 1] = acc
+        return 0
+
+    ids = lax.broadcasted_iota(jnp.int32, (heads, 128), 1)
+    everyone = rows_out + [row]
+
+    def pack_sums(j):
+        all_top = jnp.full((heads, 128), NEG, F32)
+        all_sum = jnp.zeros((heads, 128), F32)
+        for p in range(seqs // 2):
+            pair = []
+            for b in (2 * p, 2 * p + 1):
+                entry = plan[4, b]
+                total = jnp.sum(sums[entry], axis=1, keepdims=True)
+                all_top = jnp.where(ids == b, peak[b], all_top)
+                all_sum = jnp.where(ids == b, total, all_sum)
+                pair.append(run[j, entry] * (1.0 / jnp.maximum(total, 1e-30)))
+            for d in range(n):
+                mix[j, d, 2 * p * hs:2 * (p + 1) * hs, :] = jnp.concatenate(
+                    [x[d * hs:(d + 1) * hs] for x in pair], axis=0).astype(BF16)
+        if j == 0:
+            for d in range(n):
+                st[d, :hs, :] = all_top[d * hs:(d + 1) * hs]
+                st[d, hs:, :] = all_sum[d * hs:(d + 1) * hs]
+
+    ysent = {}
+
+    def to_partner(j, places):
+        for i in places:
+            r = everyone[i]
+            d = 2 * r + 1 - par
+            if j == 0:
+                ysent[2, i] = remote(st.at[d], yst.at[r], yss.at[i], ysr.at[i], {"seq": partner})
+                ysent[2, i].start()
+            ysent[j, i] = remote(mix.at[j, d], ygot.at[j, r], ys.at[j * line + i], yr.at[j * line + i], {"seq": partner})
+            ysent[j, i].start()
+
     lax.fori_loop(0, trips, third_pass, 0)
-
-    if share:
-        for k in range(2, n, 2):
-            v_copy(k).wait_recv()
-            twin_copy(k).start()
-    ids = lax.broadcasted_iota(jnp.int32, (heads, 128), 1)
-    all_top = jnp.full((heads, 128), NEG, F32)
-    all_sum = jnp.zeros((heads, 128), F32)
-    for p in range(seqs // 2):
-        pair = []
-        for b in (2 * p, 2 * p + 1):
-            entry = plan[4, b]
-            total = jnp.sum(sums[entry], axis=1, keepdims=True)
-            all_top = jnp.where(ids == b, peak[b], all_top)
-            all_sum = jnp.where(ids == b, total, all_sum)
-            pair.append(run[entry] * (1.0 / jnp.maximum(total, 1e-30)))
-        for d in range(n):
-            mix[d, 2 * p * hs:2 * (p + 1) * hs, :] = jnp.concatenate(
-                [x[d * hs:(d + 1) * hs] for x in pair], axis=0).astype(BF16)
-    for d in range(n):
-        st[d, :hs, :] = all_top[d * hs:(d + 1) * hs]
-        st[d, hs:, :] = all_sum[d * hs:(d + 1) * hs]
-
-    order = list(range(1, line)) + [0]
-    sent = []
-    for k in order:
-        r = lax.rem(row + k, line)
-        d = 2 * r + 1 - par
-        for src, dst, s, rr in ((st, yst, yss, ysr), (mix, ygot, ys, yr)):
-            copy = remote(src.at[d], dst.at[r], s.at[k], rr.at[k], {"seq": partner})
-            copy.start()
-            sent.append(copy)
-    if share:
-        for k in (1, 3):
-            v_copy(k).wait_recv()
-            twin_copy(k).start()
+    pack_sums(0)
+    to_partner(0, range(line - 1))
+    relay(peers[:line - 1][::-1])
+    lax.fori_loop(0, trips, fourth_pass, 0)
+    pack_sums(1)
+    to_partner(1, range(line - 1))
+    to_partner(0, [line - 1])
+    to_partner(1, [line - 1])
     onward = []
-    for i, k in enumerate(order):
-        sent[2 * i].wait_recv()
-        sent[2 * i + 1].wait_recv()
-        r = lax.rem(row + k, line)
+    for j, i in [(j, i) for j in range(2) for i in range(line - 1)] + [(0, line - 1), (1, line - 1)]:
+        r = everyone[i]
+        if j == 0:
+            ysent[2, i].wait_recv()
+        ysent[j, i].wait_recv()
         mine = 2 * r + par
-        o, best, total = merge(seqs, [st[mine], yst[r]], [mix[mine].astype(F32), ygot[r].astype(F32)])
-        zst[k, :hs, :] = best
-        zst[k, hs:, :] = total
-        zout[k] = o.astype(BF16)
-        if k:
-            for src, dst, s, rr in ((zst, zgst, zss, zsr), (zout, zgot, zs, zr)):
-                copy = remote(src.at[k], dst.at[k], s.at[k], rr.at[k], {"seq": lax.rem(me + 2 * k, n)})
+        columns, best, total = weigh(seqs, [st[mine], yst[r]])
+        zout[j, i] = mean(columns, [mix[j, mine], ygot[j, r]]).astype(BF16)
+        moves = [(zout.at[j, i], zgot.at[j, row], zs.at[j * line + i], zr.at[j * line + row])]
+        if j == 0:
+            zst[i, :hs, :] = best
+            zst[i, hs:, :] = total
+            moves.append((zst.at[i], zgst.at[row], zss.at[i], zsr.at[row]))
+        if i < line - 1:
+            for move in moves:
+                copy = remote(*move, {"seq": 2 * r + par})
                 copy.start()
                 onward.append(copy)
-    if share:
-        for k in range(5, n, 2):
-            v_copy(k).wait_recv()
-            twin_copy(k).start()
-    for copy in onward:
-        copy.wait_recv()
-    o, _, _ = merge(seqs, [zst[0]] + [zgst[k] for k in range(1, line)],
-                    [zout[0].astype(F32)] + [zgot[k].astype(F32) for k in range(1, line)])
-    blocks = width // 128
-    for j in range(blocks):
-        port[j] = o[:, j * 128:(j + 1) * 128]
+        relay(peers[line - 1:][i + j * (line - 1):i + j * (line - 1) + 1] if i < line - 1 else [])
+    blocks = wing // 128
+    for j in range(2):
+        for r in rows_out:
+            if j == 0:
+                remote(zst.at[0], zgst.at[r], zss.at[0], zsr.at[r], {"seq": partner}).wait_recv()
+            remote(zout.at[j, 0], zgot.at[j, r], zs.at[0], zr.at[j * line + r], {"seq": partner}).wait_recv()
+        columns, _, _ = weigh(seqs, [zst[line - 1]] + [zgst[r] for r in rows_out])
+        o = mean(columns, [zout[j, line - 1]] + [zgot[j, r] for r in rows_out])
+        for i in range(blocks):
+            port[j * blocks + i] = o[:, i * 128:(i + 1) * 128]
 
     own_v.wait()
-    for k in range(1, n):
+    for d in peers:
         if share:
-            twin_copy(k).wait_recv()
+            twin_copy(d).wait_recv()
         else:
-            v_copy(k).wait_recv()
+            v_copy(d, d).wait_recv()
     vdim = vbuf.shape[3]
     for h in range(hs):
-        x = jnp.concatenate([port[j, pl.ds(h, seqs, stride=hs), :] for j in range(blocks)], axis=1).astype(BF16)
+        x = jnp.concatenate([port[j, pl.ds(h, seqs, stride=hs), :] for j in range(2 * blocks)], axis=1).astype(BF16)
         wv = vbuf[:, h].reshape(width, vdim)
         vals[me, :, h * vdim:(h + 1) * vdim] = jnp.dot(x, wv, preferred_element_type=F32).astype(BF16)
     copies = []
-    for k in range(1, n):
-        copy = remote(vals.at[me], vals.at[me], as_.at[k], ar.at[k], {"seq": lax.rem(me + k, n)})
+    for i in [x for j in range(line - 1) for x in (line - 1 + j, j)] + [n - 2]:
+        copy = remote(vals.at[me], vals.at[me], as_.at[i], ar.at[me], {"seq": peers[i]})
         copy.start()
         copies.append(copy)
     for copy in bigw:
         copy.wait()
     rows = hs * vdim
     res = None
-    for k in range(n):
-        src = lax.rem(me - k + n, n)
-        if k:
-            copies[k - 1].wait_recv()
+    for src in [me, partner] + [peers[i] for j in range(line - 2, -1, -1) for i in (j, line - 1 + j)]:
+        if src is not me:
+            remote(vals.at[src], vals.at[src], as_.at[0], ar.at[src], {"seq": partner}).wait_recv()
         at = pl.ds(pl.multiple_of(src * rows, rows), rows)
         product = jnp.dot(vals[src], w_buf[at, :], preferred_element_type=F32)
         res = product if res is None else res + product
@@ -390,12 +418,12 @@
     tx[...] = jnp.where(first, high, low)
     copy = remote(tx, rx, ms, mr, {"mp": 1 - half})
     copy.start()
-    for c in copies + sent + onward + [x[2] for x in along] + [x[1] for x in across]:
+    for c in copies + list(ysent.values()) + onward + [x[2] for x in along] + [x[1] for x in across]:
         c.wait_send()
-    for k in range(1, n):
-        v_copy(k).wait_send()
+    for d in peers:
+        v_copy(d, me).wait_send()
         if share:
-            twin_copy(k).wait_send()
+            twin_copy(d).wait_send()
     copy.wait()
     out_ref[...] = (jnp.where(first, low, high) + rx[...]).astype(BF16)
 
@@ -444,29 +472,30 @@
             vmem((seqs, heads, 128), BF16),
             vmem((slots * (page + 8), 128), F32),
             vmem((slots, page, 128), BF16),
-            vmem((nch + 1, heads, width), F32),
+            vmem((2, nch + 1, heads, width // 2), F32),
             vmem((nch + 1, heads, 128), F32),
             vmem((nch + 1, heads, 128), F32),
             vmem((seqs, heads, 128), F32),
             vmem((nch, heads, GROUP * page), F32),
-            vmem((n, rows, width), BF16),
+            vmem((nch, heads, GROUP * page), BF16),
+            vmem((2, n, rows, width // 2), BF16),
             vmem((n, 2 * hs, 128), F32),
-            vmem((line, rows, width), BF16),
+            vmem((2, line, rows, width // 2), BF16),
             vmem((line, 2 * hs, 128), F32),
-            vmem((line, rows, width), BF16),
+            vmem((2, line, rows, width // 2), BF16),
             vmem((line, 2 * hs, 128), F32),
-            vmem((line, rows, width), BF16),
+            vmem((2, line, rows, width // 2), BF16),
             vmem((line, 2 * hs, 128), F32),
             vmem((width // 128, rows, 128), F32),
             vmem((n, hs, cols, vdim), BF16),
             vmem((n, seqs, hs * vdim), BF16),
             vmem((seqs, wide // 2), F32),
             vmem((seqs, wide // 2), F32),
-            dma((8,)), dma((2 * bulk,)),
+            dma((7 + QPARTS,)), dma((2 * bulk,)),
             dma((QPARTS * line,)), dma((QPARTS * line,)), dma((QPARTS * line,)), dma((QPARTS * line,)),
             dma((n,)), dma((n,)), dma((n,)), dma((n,)),
-            dma((line,)), dma((line,)), dma((line,)), dma((line,)),
-            dma((line,)), dma((line,)), dma((line,)), dma((line,)),
+            dma((2 * line,)), dma((2 * line,)), dma((line,)), dma((line,)),
+            dma((2 * line,)), dma((2 * line,)), dma((line,)), dma((line,)),
             dma((n,)), dma((n,)), dma, dma,
         ],
         compiler_params=pltpu.CompilerParams(

time: 46.1 us -> 42.3 us (0.918)
  Pallas kernels: 44.6 us -> 40.8 us
    pallas_call x1, Pallas kernels: 44.6 us -> 40.8 us  [local(): pl.pallas_call(functools.partial(kernel, n, groups, pack, scale, nch), ou...]
where the time goes in v3:
time: 42.3 us; the launch traced here: 42.1 us
  Pallas kernels  40.8 us (96%)
  local copies, waits for them, and re-layouts  1.3 us (3%)
    pallas_call x1, Pallas kernels, local(): pl.pallas_call(functools.partial(kernel, n, groups, pack, scale, nch), ou...  40.8 us
    unnamed x1, local copies, waits for them, and re-layouts  1.3 us

profile of v3, /device:TPU:0, one launch (start us, length us, event | category | flops | bytes accessed | tf_op | source)
XLA Modules:
  0.0 42.1 jit_solution(13994068591642253992)
XLA Ops:
  0.0 40.8 %decode.1 = bf16[8,448]{1,0:T(8,128)(2,1)} custom-call(s32[8]{0:T(128)} %lengths_hbm.1, s32[8,256]{1,0:T(8,128)} %table_hbm.1, bf16[128,4096]{1,0:T(8,128)(2,1)} %rope_hbm.1, bf16[8,64,128]{2,1,0:T(8,128)(2,1)} %qn_hbm.1, bf16[64,64,128]{2,1,0:T(8,128)(2,1)} %bitcast.1, bf16[8,64,64]{2,1,0:T(8,128)(2,1)} %qr_hbm.1, bf16[128,64,512]{2,1,0:T(8,128)(2,1)} %lat_hbm.1, ...), custom_call_target="tpu_custom_call" | custom-call | tf_op jit(solution)/shard_map/decode/pallas_call | solution.py:452
  40.8 1.3 %copy.11 = bf16[8,448]{1,0:T(8,128)(2,1)} copy(bf16[8,448]{1,0:T(8,128)(2,1)} %decode.1) | data formatting | bytes 14336

commit v4 on v3

--- a/solution.py
+++ b/solution.py
@@ -11,8 +11,8 @@
 NEG = -1e30
 MESH = pl.DeviceIdType.MESH
 GROUP = 4
-UNROLL = 20
-UNROLL1 = 10
+UNROLL = 19
+UNROLL1 = 19
 QPARTS = 2
 F32 = jnp.float32
 BF16 = jnp.bfloat16
@@ -499,7 +499,7 @@
             dma((n,)), dma((n,)), dma, dma,
         ],
         compiler_params=pltpu.CompilerParams(
-            has_side_effects=True, collective_id=1, vmem_limit_bytes=60 * 1024 * 1024),
+            has_side_effects=True, collective_id=1, vmem_limit_bytes=55216 * 1024),
         name="decode",
     )(lengths, page_table, rope_cache, q_nope, w_uk.transpose(0, 2, 1), q_rope, latent_cache, value_up_weight, w_out)
 

time: 42.3 us -> 41.5 us (0.981)
  Pallas kernels: 40.8 us -> 40.1 us
    pallas_call x1, Pallas kernels: 40.8 us -> 40.1 us  [local(): pl.pallas_call(functools.partial(kernel, n, groups, pack, scale, nch), ou...]
    unnamed x1 -> x3, local copies, waits for them, and re-layouts: 1.3 us -> 1.26 us
where the time goes in v4:
time: 41.5 us; the launch traced here: 41.3 us
  Pallas kernels  40.1 us (97%)
  local copies, waits for them, and re-layouts  1.26 us (3%)
    pallas_call x1, Pallas kernels, local(): pl.pallas_call(functools.partial(kernel, n, groups, pack, scale, nch), ou...  40.1 us
    unnamed x3, local copies, waits for them, and re-layouts  1.26 us

profile of v4, /device:TPU:0, one launch (start us, length us, event | category | flops | bytes accessed | tf_op | source)
XLA Modules:
  0.0 41.3 jit_solution(1353860884802652204)
XLA Ops:
  0.0 0.0 copy-start
  0.0 0.7 %copy-done = s32[8]{0:T(128)S(1)} copy-done((s32[8]{0:T(128)S(1)}, s32[8]{0:T(128)}, u32[]{:S(2)}) %copy-start) | copy-done | bytes 56
  0.7 40.1 %decode.1 = bf16[8,448]{1,0:T(8,128)(2,1)S(1)} custom-call(s32[8]{0:T(128)S(1)} %copy-done, s32[8,256]{1,0:T(8,128)} %table_hbm.1, bf16[128,4096]{1,0:T(8,128)(2,1)} %rope_hbm.1, bf16[8,64,128]{2,1,0:T(8,128)(2,1)} %qn_hbm.1, bf16[64,64,128]{2,1,0:T(8,128)(2,1)} %bitcast.1, bf16[8,64,64]{2,1,0:T(8,128)(2,1)} %qr_hbm.1, bf16[128,64,512]{2,1,0:T(8,128)(2,1)} %lat_hbm.1, ...), custom_call_target="tpu_custom_call" | custom-call | tf_op jit(solution)/shard_map/decode/pallas_call | solution.py:452
  40.7 0.6 %copy.11 = bf16[8,448]{1,0:T(8,128)(2,1)} copy(bf16[8,448]{1,0:T(8,128)(2,1)S(1)} %decode.1) | data formatting | bytes 14336
Async XLA Ops:
  0.0 0.7 %copy-start = (s32[8]{0:T(128)S(1)}, s32[8]{0:T(128)}, u32[]{:S(2)}) copy-start(s32[8]{0:T(128)} %lengths_hbm.1) | copy-start | bytes 100

commit v5 on v4

--- a/solution.py
+++ b/solution.py
@@ -11,7 +11,7 @@
 NEG = -1e30
 MESH = pl.DeviceIdType.MESH
 GROUP = 4
-UNROLL = 19
+UNROLL = 38
 UNROLL1 = 19
 QPARTS = 2
 F32 = jnp.float32

time: 41.5 us -> 41.5 us (level)
  no operation moved by 1% of the time
where the time goes in v5:
time: 41.5 us; the launch traced here: 41.4 us
  Pallas kernels  40.1 us (97%)
  local copies, waits for them, and re-layouts  1.26 us (3%)
    pallas_call x1, Pallas kernels, local(): pl.pallas_call(functools.partial(kernel, n, groups, pack, scale, nch), ou...  40.1 us
    unnamed x3, local copies, waits for them, and re-layouts  1.26 us

profile of v5, /device:TPU:0, one launch (start us, length us, event | category | flops | bytes accessed | tf_op | source)
XLA Modules:
  0.0 41.4 jit_solution(4980183989661944994)
XLA Ops:
  0.0 0.0 copy-start
  0.0 0.7 %copy-done = s32[8]{0:T(128)S(1)} copy-done((s32[8]{0:T(128)S(1)}, s32[8]{0:T(128)}, u32[]{:S(2)}) %copy-start) | copy-done | bytes 56
  0.7 40.1 %decode.1 = bf16[8,448]{1,0:T(8,128)(2,1)S(1)} custom-call(s32[8]{0:T(128)S(1)} %copy-done, s32[8,256]{1,0:T(8,128)} %table_hbm.1, bf16[128,4096]{1,0:T(8,128)(2,1)} %rope_hbm.1, bf16[8,64,128]{2,1,0:T(8,128)(2,1)} %qn_hbm.1, bf16[64,64,128]{2,1,0:T(8,128)(2,1)} %bitcast.1, bf16[8,64,64]{2,1,0:T(8,128)(2,1)} %qr_hbm.1, bf16[128,64,512]{2,1,0:T(8,128)(2,1)} %lat_hbm.1, ...), custom_call_target="tpu_custom_call" | custom-call | tf_op jit(solution)/shard_map/decode/pallas_call | solution.py:452
  40.8 0.6 %copy.11 = bf16[8,448]{1,0:T(8,128)(2,1)} copy(bf16[8,448]{1,0:T(8,128)(2,1)S(1)} %decode.1) | data formatting | bytes 14336
Async XLA Ops:
  0.0 0.7 %copy-start = (s32[8]{0:T(128)S(1)}, s32[8]{0:T(128)}, u32[]{:S(2)}) copy-start(s32[8]{0:T(128)} %lengths_hbm.1) | copy-start | bytes 100
